TPU v7x, 32 devices: a whole 2x2x4 slice. The times are simulated.
32 devices in a mesh: rep: 8 (over y, x, core), sp: 4 (over z).
Axes of the slice: x: 2, y: 2, z: 4, core: 2. Of those that a mesh axis runs over, the one named last changes fastest.
Arguments:
- field: bfloat16 [8, 128, 100, 128], P('rep', 'sp'), may hold values from -6 to 6
- send_blocks: int32 [4, 4, 8], P('sp'), may hold values from 0 to 31
- send_count: int32 [4, 4], P('sp'), may hold values from 1 to 8, as said below
- regrid_weights: bfloat16 [32, 8, 128, 128], P('sp'), may hold values from -0.1875 to 0.1875
- tile_slot: int32 [32, 8], P('sp'), may hold values from 0 to 31
- edge_inputs: bfloat16 [12288, 1536], P(('rep', 'sp')), may hold values from -6 to 6
- cotangent: bfloat16 [12288, 512], P(('rep', 'sp')), may hold values from -0.15625 to 0.15625
Outputs:
- hidden: bfloat16 [8, 32, 100, 128], P('rep', 'sp')
- weight_grad: float32 [1536, 512], P(('rep', 'sp'))
Inputs may be any that keep to these rules, and one draw needn't show every extreme that they name: `send_count`: every count is at most 8, and some pair of shards has exactly 8 in every draw.
All inputs are finite; a program needn't handle non-finite values.
Results may differ from a plain program's by a relative error of at most 0.001.
Values may be sent and summed in bfloat16 or wider, within the bound.
A program may use at most 64 MiB of HBM per device.

v0:
```python
import jax
import jax.numpy as jnp
from jax import lax
from jax.experimental import pallas as pl
from jax.experimental.pallas import tpu as pltpu
from jax.sharding import PartitionSpec as P

MESH = pl.DeviceIdType.MESH


def body(field, send_blocks, send_count, regrid_weights, tile_slot, edge_inputs, cotangent):
    sample = field[0]
    own_lists = send_blocks[0]
    shards = own_lists.shape[0]
    slots_each = own_lists.shape[1]
    channels = sample.shape[1]
    cells = sample.shape[2]
    alive = jnp.arange(slots_each, dtype=jnp.int32)[None, :] < send_count[0][:, None]
    outgoing = jnp.where(alive[:, :, None, None], sample[own_lists], jnp.zeros((), jnp.bfloat16))
    incoming = lax.all_to_all(outgoing, "sp", split_axis=0, concat_axis=0, tiled=True)
    block_pool = incoming.reshape(shards * slots_each, channels, cells)
    picked = block_pool[tile_slot]
    hidden = jnp.einsum(
        "tbcx,tbxn->tcn", picked, regrid_weights, preferred_element_type=jnp.float32
    )
    hidden = hidden.astype(jnp.bfloat16)[None]
    partial_value = lax.psum_scatter(
        lax.dot_general(
            edge_inputs, cotangent, (((0,), (0,)), ((), ())), preferred_element_type=jnp.float32
        ),
        "rep",
        scatter_dimension=0,
        tiled=True,
    )
    weight_grad = lax.psum_scatter(partial_value, "sp", scatter_dimension=0, tiled=True)
    return (hidden, weight_grad)


def kernel(
    lists, counts, slots, field_hbm, weights_hbm, edge_hbm, cot_hbm,
    hidden_out, grad_out,
    field, wide, weights, edge, cot, outgoing, pool, tall, part, got1, got2, got3, gotz, gotf,
    load_sem, a2a_send, a2a_recv, s1, r1, s2, r2, s3, r3, sz, rz, sf, rf,
):
    rep = lax.axis_index("rep")
    me = lax.axis_index("sp")
    core = rep % 2
    x = (rep // 2) % 2
    y = rep // 4
    w1, w2 = 1 + core, 2 - core
    b1 = x + core * (y - x)
    b2 = y + core * (x - y)
    twin = rep + 1 - 2 * core
    first = rep + (1 - 2 * b1) * 2 * w1
    second = rep + (1 - 2 * b2) * 2 * w2
    low, high = me % 2, me // 2
    near = 2 * high + 1 - low
    far = 2 * (1 - high) + low
    diag = 2 * (1 - high) + 1 - low
    channels, blocks, cells = field.shape
    slots_each = lists.shape[2]
    tiles, reads = slots.shape
    width = edge_hbm.shape[1] // 4

    loads = [
        pltpu.make_async_copy(field_hbm.at[0], field, load_sem.at[0]),
        pltpu.make_async_copy(edge_hbm, edge, load_sem.at[1]),
        pltpu.make_async_copy(cot_hbm, cot, load_sem.at[2]),
        pltpu.make_async_copy(weights_hbm, weights, load_sem.at[3]),
    ]
    for load in loads:
        load.start()

    barrier = pltpu.get_barrier_semaphore()
    sp_peers = [far, diag, near]
    for peer in sp_peers:
        pl.semaphore_signal(barrier, inc=1, device_id=(rep, peer), device_id_type=MESH)
    for peer in (twin, first, second):
        pl.semaphore_signal(barrier, inc=1, device_id=(peer, me), device_id_type=MESH)

    loads[0].wait()
    wide[...] = field[...].astype(jnp.float32).reshape(wide.shape)

    def block_for(d, j):
        block = wide[pl.ds(lists[0, d, j], channels, stride=blocks), :]
        block = jnp.where(j < counts[0, d], block, jnp.zeros_like(block))
        return block.astype(jnp.bfloat16)

    def send(src, dst, ssem, rsem, device):
        copy = pltpu.make_async_remote_copy(
            src_ref=src, dst_ref=dst, send_sem=ssem, recv_sem=rsem,
            device_id=device, device_id_type=MESH,
        )
        copy.start()
        return copy

    a2a = []
    for k, peer in enumerate(sp_peers):
        for j in range(slots_each):
            outgoing[k, j] = block_for(peer, j)
        if k == 0:
            pl.semaphore_wait(barrier, 6)
        a2a.append(send(
            outgoing.at[k], pool.at[pl.ds(me * slots_each, slots_each)],
            a2a_send.at[k], a2a_recv.at[k], (rep, peer),
        ))

    def chunk(flip1, flip2):
        return (b1 + flip1 * (1 - 2 * b1)) * w1 + (b2 + flip2 * (1 - 2 * b2)) * w2

    loads[1].wait()
    loads[2].wait()
    to_twin = []
    for k, (f1, f2) in enumerate(((1, 1), (0, 1), (1, 0), (0, 0))):
        q = chunk(f1, f2)
        columns = pl.ds(pl.multiple_of(q * width, 128), width)
        value = lax.dot_general(
            edge[:, columns], cot[...], (((0,), (0,)), ((), ())),
            preferred_element_type=jnp.float32,
        )
        part[q] = value.reshape(part.shape[1:])
        to_twin.append(send(
            part.at[q, 1 - core], got1.at[k], s1.at[k], r1.at[k], (twin, me)
        ))
    for j in range(slots_each):
        pool[me * slots_each + j] = block_for(me, j)

    order = [diag, near, far, me]
    c_both, c_first, c_second, c_none = chunk(1, 1), chunk(1, 0), chunk(0, 1), chunk(0, 0)

    def fold(q, k):
        to_twin[k].wait_recv()
        part[q, core] = part[q, core] + got1[k]

    out2 = []
    for k, q in enumerate((c_both, c_first)):
        fold(q, k)
        for i in range(4):
            out2.append(send(
                part.at[q, core, order[i]], got2.at[k, order[i]],
                s2.at[k, i], r2.at[k, i], (first, me),
            ))
    fold(c_second, 2)
    fold(c_none, 3)
    out3 = []
    for i in range(4):
        out2[i].wait_recv()
        part[c_second, core, order[i]] = part[c_second, core, order[i]] + got2[0, order[i]]
        out3.append(send(
            part.at[c_second, core, order[i]], got3.at[order[i]],
            s3.at[i], r3.at[i], (second, me),
        ))
    outz = []
    for i in range(4):
        out2[4 + i].wait_recv()
        out3[i].wait_recv()
        total = part[c_none, core, order[i]] + got2[1, order[i]] + got3[order[i]]
        part[c_none, core, order[i]] = total
        if i < 2:
            outz.append(send(
                part.at[c_none, core, order[i]], gotz.at[i], sz.at[i], rz.at[i], (rep, near)
            ))
    outz[0].wait_recv()
    part[c_none, core, far] = part[c_none, core, far] + gotz[0]
    last = send(part.at[c_none, core, far], gotf, sf, rf, (rep, far))

    for copy in a2a:
        copy.wait_recv()
    loads[3].wait()
    for t in range(tiles):
        left = jnp.concatenate([pool[slots[t, b]] for b in range(reads)], axis=1)
        right = weights[t].reshape(reads * weights.shape[2], weights.shape[3])
        tall[pl.ds(t, channels, stride=tiles), :] = jnp.dot(
            left, right, preferred_element_type=jnp.float32
        )
    hidden_out[0] = tall[...].reshape(hidden_out.shape[1:]).astype(hidden_out.dtype)

    outz[1].wait_recv()
    total = part[c_none, core, me] + gotz[1]
    last.wait_recv()
    grad_out[...] = total + gotf[...]
    for copy in a2a + to_twin + out2 + out3 + outz + [last]:
        copy.wait_send()


def settle(hidden, grad, hidden_out, grad_out, hidden_held, grad_held, sem):
    pairs = ((hidden, hidden_held, hidden_out), (grad, grad_held, grad_out))
    inward = [pltpu.make_async_copy(a, b, sem.at[0, i]) for i, (a, b, _) in enumerate(pairs)]
    outward = [pltpu.make_async_copy(b, c, sem.at[1, i]) for i, (_, b, c) in enumerate(pairs)]
    for copy in inward:
        copy.start()
    for i in range(2):
        inward[i].wait()
        outward[i].start()
    for copy in outward:
        copy.wait()


def fused(field, send_blocks, send_count, regrid_weights, tile_slot, edge_inputs, cotangent):
    _, blocks, channels, cells = field.shape
    slots_each = send_blocks.shape[2]
    tiles = tile_slot.shape[0]
    nodes = regrid_weights.shape[3]
    n_in, hid = edge_inputs.shape[1], cotangent.shape[1]
    rows = n_in // (lax.axis_size("rep") * lax.axis_size("sp"))
    bf16, f32 = jnp.bfloat16, jnp.float32
    dma = pltpu.SemaphoreType.DMA
    smem = pl.BlockSpec(memory_space=pltpu.SMEM)
    far = pl.BlockSpec(memory_space=pl.ANY)
    near = pl.BlockSpec(memory_space=pltpu.VMEM)
    out_shape = (
        jax.ShapeDtypeStruct((1, channels, tiles, nodes), bf16),
        jax.ShapeDtypeStruct((rows, hid), f32),
    )
    hidden, grad = pl.pallas_call(
        kernel,
        out_shape=out_shape,
        in_specs=[smem, smem, smem, far, far, far, far],
        out_specs=(near, near),
        scratch_shapes=[
            pltpu.VMEM((channels, blocks, cells), bf16),
            pltpu.VMEM((channels * blocks, cells), f32),
            pltpu.VMEM(regrid_weights.shape, bf16),
            pltpu.VMEM(edge_inputs.shape, bf16),
            pltpu.VMEM(cotangent.shape, bf16),
            pltpu.VMEM((3, slots_each, channels, cells), bf16),
            pltpu.VMEM((4 * slots_each, channels, cells), bf16),
            pltpu.VMEM((channels * tiles, nodes), f32),
            pltpu.VMEM((4, 2, 4, rows, hid), f32),
            pltpu.VMEM((4, 4, rows, hid), f32),
            pltpu.VMEM((2, 4, rows, hid), f32),
            pltpu.VMEM((4, rows, hid), f32),
            pltpu.VMEM((2, rows, hid), f32),
            pltpu.VMEM((rows, hid), f32),
            dma((4,)),
            dma((3,)), dma((3,)),
            dma((4,)), dma((4,)),
            dma((2, 4)), dma((2, 4)),
            dma((4,)), dma((4,)),
            dma((2,)), dma((2,)),
            dma, dma,
        ],
        compiler_params=pltpu.CompilerParams(
            collective_id=0, has_side_effects=True, vmem_limit_bytes=56 * 1024 * 1024
        ),
    )(
        send_blocks, send_count, tile_slot, jnp.transpose(field, (0, 2, 1, 3)),
        regrid_weights, edge_inputs, cotangent,
    )
    hidden, grad = pl.pallas_call(
        settle, out_shape=out_shape, in_specs=[far, far], out_specs=(far, far),
        scratch_shapes=[
            pltpu.VMEM(out_shape[0].shape, bf16), pltpu.VMEM(out_shape[1].shape, f32), dma((2, 2)),
        ],
        compiler_params=pltpu.CompilerParams(vmem_limit_bytes=57000 * 1024),
    )(hidden, grad)
    return jnp.transpose(hidden, (0, 2, 1, 3)), grad


def solution(mesh):
    in_specs = (
        P("rep", "sp", None, None),
        P("sp", None, None),
        P("sp", None),
        P("sp", None, None, None),
        P("sp", None),
        P(("rep", "sp"), None),
        P(("rep", "sp"), None),
    )
    out_specs = (P("rep", "sp", None, None), P(("rep", "sp"), None))
    binary = mesh.shape["rep"] == 2 * 2 * 2 and mesh.shape["sp"] == 2 * 2
    inner = fused if binary else body
    return jax.shard_map(inner, mesh=mesh, in_specs=in_specs, out_specs=out_specs, check_vma=False)
```

profile of v0, /device:TPU:0, one launch (start us, length us, event | category | flops | bytes accessed | tf_op | source)
XLA Modules:
  0.0 33.2 jit_solution(12386815079336845185)
XLA Ops:
  0.6 30.9 %shard_map.86 = (bf16[1,100,8,128]{3,2,1,0:T(8,128)(2,1)}, f32[48,512]{1,0:T(8,128)}) custom-call(s32[1,4,8]{2,1,0:T(4,128)} %lists.1, s32[1,4]{1,0:T(1,128)} %counts.1, s32[8,8]{1,0:T(8,128)} %slots.1, bf16[1,100,32,128]{3,2,1,0:T(8,128)(2,1)} %bitcast.2, bf16[8,8,128,128]{3,2,1,0:T(8,128)(2,1)} %weights_hbm.1, bf16[384,1536]{1,0:T(8,128)(2,1)} %edge_hbm.1, ...), custom_call_target="tpu_custom_call" | custom-call | tf_op jit(solution)/shard_map/pallas_call | solution.py:215
  31.5 1.7 %shard_map.87 = (bf16[1,100,8,128]{3,2,1,0:T(8,128)(2,1)}, f32[48,512]{1,0:T(8,128)}) custom-call(bf16[1,100,8,128]{3,2,1,0:T(8,128)(2,1)} %get-tuple-element.6.hidden, f32[48,512]{1,0:T(8,128)} %get-tuple-element.7.grad), custom_call_target="tpu_custom_call" | custom-call | tf_op jit(solution)/shard_map/pallas_call | solution.py:250
where the time goes:
time: 33.4 us; the launch traced here: 33.2 us
  Pallas kernels  32.5 us (97%)
  between operations  0.64 us (2%)
    pallas_call x1, Pallas kernels, fused(): pl.pallas_call(kernel, out_shape=out_shape, in_specs=[smem, smem, smem, f...  30.9 us
    pallas_call x1, Pallas kernels, fused(): pl.pallas_call(settle, out_shape=out_shape, in_specs=[far, far], out_spec...  1.67 us

commit v1 on v0

--- a/solution.py
+++ b/solution.py
@@ -36,10 +36,19 @@
     return (hidden, weight_grad)
 
 
+def encode(value):
+    return value
+
+
+def decode(code):
+    return code
+
+
 def kernel(
-    lists, counts, slots, field_hbm, weights_hbm, edge_hbm, cot_hbm,
+    lists_hbm, counts_hbm, slots_hbm, field_hbm, weights_hbm, edge_hbm, cot_hbm,
     hidden_out, grad_out,
-    field, wide, weights, edge, cot, outgoing, pool, tall, part, got1, got2, got3, gotz, gotf,
+    lists, counts, slots, field, wide, weights, edge, cot, outgoing, pool, tall, hidden, grad,
+    part, got1, link2, got2, link3, got3, linkz, gotz, linkf, gotf,
     load_sem, a2a_send, a2a_recv, s1, r1, s2, r2, s3, r3, sz, rz, sf, rf,
 ):
     rep = lax.axis_index("rep")
@@ -57,59 +66,74 @@
     near = 2 * high + 1 - low
     far = 2 * (1 - high) + low
     diag = 2 * (1 - high) + 1 - low
+    outer, inner = 3 * (1 - high), 2 - high
     channels, blocks, cells = field.shape
+    pitch = wide.shape[1]
     slots_each = lists.shape[2]
     tiles, reads = slots.shape
     width = edge_hbm.shape[1] // 4
+    pieces = 2
+    piece = slots_each // pieces
 
     loads = [
         pltpu.make_async_copy(field_hbm.at[0], field, load_sem.at[0]),
+        pltpu.make_async_copy(lists_hbm, lists, load_sem.at[4]),
+        pltpu.make_async_copy(counts_hbm, counts, load_sem.at[5]),
         pltpu.make_async_copy(edge_hbm, edge, load_sem.at[1]),
         pltpu.make_async_copy(cot_hbm, cot, load_sem.at[2]),
+        pltpu.make_async_copy(slots_hbm, slots, load_sem.at[6]),
         pltpu.make_async_copy(weights_hbm, weights, load_sem.at[3]),
     ]
     for load in loads:
         load.start()
+    field_load, lists_load, counts_load, edge_load, cot_load, slots_load, weights_load = loads
 
     barrier = pltpu.get_barrier_semaphore()
-    sp_peers = [far, diag, near]
-    for peer in sp_peers:
+    for peer in (far, diag, near):
         pl.semaphore_signal(barrier, inc=1, device_id=(rep, peer), device_id_type=MESH)
     for peer in (twin, first, second):
         pl.semaphore_signal(barrier, inc=1, device_id=(peer, me), device_id_type=MESH)
 
-    loads[0].wait()
-    wide[...] = field[...].astype(jnp.float32).reshape(wide.shape)
+    field_load.wait()
+    wide[:, :blocks, :] = field[...].astype(jnp.float32)
+    rows = wide.reshape(channels * pitch, cells)
+    lists_load.wait()
+    counts_load.wait()
 
     def block_for(d, j):
-        block = wide[pl.ds(lists[0, d, j], channels, stride=blocks), :]
+        block = rows[pl.ds(lists[0, d, j], channels, stride=pitch), :]
         block = jnp.where(j < counts[0, d], block, jnp.zeros_like(block))
         return block.astype(jnp.bfloat16)
 
-    def send(src, dst, ssem, rsem, device):
-        copy = pltpu.make_async_remote_copy(
+    def remote(src, dst, ssem, rsem, device):
+        return pltpu.make_async_remote_copy(
             src_ref=src, dst_ref=dst, send_sem=ssem, recv_sem=rsem,
             device_id=device, device_id_type=MESH,
         )
+
+    def send(*args):
+        copy = remote(*args)
         copy.start()
         return copy
 
     a2a = []
-    for k, peer in enumerate(sp_peers):
-        for j in range(slots_each):
-            outgoing[k, j] = block_for(peer, j)
-        if k == 0:
-            pl.semaphore_wait(barrier, 6)
-        a2a.append(send(
-            outgoing.at[k], pool.at[pl.ds(me * slots_each, slots_each)],
-            a2a_send.at[k], a2a_recv.at[k], (rep, peer),
-        ))
+    for k, peer in enumerate((outer, near, inner)):
+        for h in range(pieces):
+            for j in range(h * piece, (h + 1) * piece):
+                outgoing[k, j] = block_for(peer, j)
+            if k == 0 and h == 0:
+                pl.semaphore_wait(barrier, 6)
+            a2a.append(send(
+                outgoing.at[k, pl.ds(h * piece, piece)],
+                pool.at[pl.ds(me * slots_each + h * piece, piece)],
+                a2a_send.at[k, h], a2a_recv.at[me, h], (rep, peer),
+            ))
 
     def chunk(flip1, flip2):
         return (b1 + flip1 * (1 - 2 * b1)) * w1 + (b2 + flip2 * (1 - 2 * b2)) * w2
 
-    loads[1].wait()
-    loads[2].wait()
+    edge_load.wait()
+    cot_load.wait()
     to_twin = []
     for k, (f1, f2) in enumerate(((1, 1), (0, 1), (1, 0), (0, 0))):
         q = chunk(f1, f2)
@@ -118,69 +142,78 @@
             edge[:, columns], cot[...], (((0,), (0,)), ((), ())),
             preferred_element_type=jnp.float32,
         )
-        part[q] = value.reshape(part.shape[1:])
+        part[k] = value.reshape(part.shape[1:])
         to_twin.append(send(
-            part.at[q, 1 - core], got1.at[k], s1.at[k], r1.at[k], (twin, me)
+            part.at[k, 1 - core], got1.at[k], s1.at[k], r1.at[k], (twin, me)
         ))
     for j in range(slots_each):
         pool[me * slots_each + j] = block_for(me, j)
 
     order = [diag, near, far, me]
-    c_both, c_first, c_second, c_none = chunk(1, 1), chunk(1, 0), chunk(0, 1), chunk(0, 0)
-
-    def fold(q, k):
-        to_twin[k].wait_recv()
-        part[q, core] = part[q, core] + got1[k]
+    both, crossed, after, kept = (0, 0), (2, 1), (1, 2), (3, 3)
+
+    def folded(mine, theirs, i):
+        return part[mine, core, order[i]] + got1[theirs, order[i]]
 
     out2 = []
-    for k, q in enumerate((c_both, c_first)):
-        fold(q, k)
+    for n, k in enumerate((both, crossed)):
+        to_twin[k[1]].wait_recv()
         for i in range(4):
+            link2[n, i] = encode(folded(*k, i))
             out2.append(send(
-                part.at[q, core, order[i]], got2.at[k, order[i]],
-                s2.at[k, i], r2.at[k, i], (first, me),
+                link2.at[n, i], got2.at[n, i], s2.at[n, i], r2.at[n, i], (first, me)
             ))
-    fold(c_second, 2)
-    fold(c_none, 3)
+    to_twin[after[1]].wait_recv()
     out3 = []
     for i in range(4):
+        value = folded(*after, i)
         out2[i].wait_recv()
-        part[c_second, core, order[i]] = part[c_second, core, order[i]] + got2[0, order[i]]
-        out3.append(send(
-            part.at[c_second, core, order[i]], got3.at[order[i]],
-            s3.at[i], r3.at[i], (second, me),
-        ))
+        link3[i] = encode(value + decode(got2[0, i]))
+        out3.append(send(link3.at[i], got3.at[i], s3.at[i], r3.at[i], (second, me)))
+    to_twin[kept[1]].wait_recv()
     outz = []
+    totals = []
     for i in range(4):
+        value = folded(*kept, i)
         out2[4 + i].wait_recv()
+        value = value + decode(got2[1, i])
         out3[i].wait_recv()
-        total = part[c_none, core, order[i]] + got2[1, order[i]] + got3[order[i]]
-        part[c_none, core, order[i]] = total
+        value = value + decode(got3[i])
         if i < 2:
-            outz.append(send(
-                part.at[c_none, core, order[i]], gotz.at[i], sz.at[i], rz.at[i], (rep, near)
-            ))
+            linkz[i] = encode(value)
+            outz.append(send(linkz.at[i], gotz.at[i], sz.at[i], rz.at[i], (rep, near)))
+        else:
+            part[kept[0], core, order[i]] = value
     outz[0].wait_recv()
-    part[c_none, core, far] = part[c_none, core, far] + gotz[0]
-    last = send(part.at[c_none, core, far], gotf, sf, rf, (rep, far))
-
-    for copy in a2a:
-        copy.wait_recv()
-    loads[3].wait()
+    linkf[...] = encode(part[kept[0], core, far] + decode(gotz[0]))
+    last = send(linkf, gotf, sf, rf, (rep, far))
+    outz[1].wait_recv()
+    grad[...] = part[kept[0], core, me] + decode(gotz[1])
+
+    slots_load.wait()
+    weights_load.wait()
+    for peer in (near, far, diag):
+        for h in range(pieces):
+            ready = pool.at[pl.ds(peer * slots_each + h * piece, piece)]
+            remote(ready, ready, a2a_send.at[0, h], a2a_recv.at[peer, h], (rep, peer)).wait_recv()
     for t in range(tiles):
         left = jnp.concatenate([pool[slots[t, b]] for b in range(reads)], axis=1)
         right = weights[t].reshape(reads * weights.shape[2], weights.shape[3])
         tall[pl.ds(t, channels, stride=tiles), :] = jnp.dot(
             left, right, preferred_element_type=jnp.float32
         )
-    hidden_out[0] = tall[...].reshape(hidden_out.shape[1:]).astype(hidden_out.dtype)
-
-    outz[1].wait_recv()
-    total = part[c_none, core, me] + gotz[1]
+    hidden[...] = tall[...].reshape(hidden.shape).astype(hidden.dtype)
+    hidden_store = pltpu.make_async_copy(hidden, hidden_out.at[0], load_sem.at[0])
+    hidden_store.start()
+
     last.wait_recv()
-    grad_out[...] = total + gotf[...]
+    grad[...] = grad[...] + decode(gotf[...])
+    grad_store = pltpu.make_async_copy(grad, grad_out, load_sem.at[1])
+    grad_store.start()
     for copy in a2a + to_twin + out2 + out3 + outz + [last]:
         copy.wait_send()
+    hidden_store.wait()
+    grad_store.wait()
 
 
 def settle(hidden, grad, hidden_out, grad_out, hidden_held, grad_held, sem):
@@ -205,9 +238,8 @@
     rows = n_in // (lax.axis_size("rep") * lax.axis_size("sp"))
     bf16, f32 = jnp.bfloat16, jnp.float32
     dma = pltpu.SemaphoreType.DMA
-    smem = pl.BlockSpec(memory_space=pltpu.SMEM)
+    i32, link = jnp.int32, jnp.float32
     far = pl.BlockSpec(memory_space=pl.ANY)
-    near = pl.BlockSpec(memory_space=pltpu.VMEM)
     out_shape = (
         jax.ShapeDtypeStruct((1, channels, tiles, nodes), bf16),
         jax.ShapeDtypeStruct((rows, hid), f32),
@@ -215,25 +247,34 @@
     hidden, grad = pl.pallas_call(
         kernel,
         out_shape=out_shape,
-        in_specs=[smem, smem, smem, far, far, far, far],
-        out_specs=(near, near),
+        in_specs=[far] * 7,
+        out_specs=(far, far),
         scratch_shapes=[
+            pltpu.SMEM(send_blocks.shape, i32),
+            pltpu.SMEM(send_count.shape, i32),
+            pltpu.SMEM(tile_slot.shape, i32),
             pltpu.VMEM((channels, blocks, cells), bf16),
-            pltpu.VMEM((channels * blocks, cells), f32),
+            pltpu.VMEM((channels, blocks + 8, cells), f32),
             pltpu.VMEM(regrid_weights.shape, bf16),
             pltpu.VMEM(edge_inputs.shape, bf16),
             pltpu.VMEM(cotangent.shape, bf16),
             pltpu.VMEM((3, slots_each, channels, cells), bf16),
             pltpu.VMEM((4 * slots_each, channels, cells), bf16),
             pltpu.VMEM((channels * tiles, nodes), f32),
+            pltpu.VMEM((channels, tiles, nodes), bf16),
+            pltpu.VMEM((rows, hid), f32),
             pltpu.VMEM((4, 2, 4, rows, hid), f32),
             pltpu.VMEM((4, 4, rows, hid), f32),
-            pltpu.VMEM((2, 4, rows, hid), f32),
-            pltpu.VMEM((4, rows, hid), f32),
-            pltpu.VMEM((2, rows, hid), f32),
-            pltpu.VMEM((rows, hid), f32),
-            dma((4,)),
-            dma((3,)), dma((3,)),
+            pltpu.VMEM((2, 4, rows, hid), link),
+            pltpu.VMEM((2, 4, rows, hid), link),
+            pltpu.VMEM((4, rows, hid), link),
+            pltpu.VMEM((4, rows, hid), link),
+            pltpu.VMEM((2, rows, hid), link),
+            pltpu.VMEM((2, rows, hid), link),
+            pltpu.VMEM((rows, hid), link),
+            pltpu.VMEM((rows, hid), link),
+            dma((7,)),
+            dma((3, 2)), dma((4, 2)),
             dma((4,)), dma((4,)),
             dma((2, 4)), dma((2, 4)),
             dma((4,)), dma((4,)),

time: 33.4 us -> 32.3 us (0.967)
  Pallas kernels: 32.5 us -> 31.5 us
    pallas_call x1, Pallas kernels: 30.9 us -> 29.8 us  [fused(): pl.pallas_call(kernel, out_shape=out_shape, in_specs=[far] * 7, out_specs...]
where the time goes in v1:
time: 32.3 us; the launch traced here: 32.1 us
  Pallas kernels  31.5 us (98%)
  between operations  0.64 us (2%)
    pallas_call x1, Pallas kernels, fused(): pl.pallas_call(kernel, out_shape=out_shape, in_specs=[far] * 7, out_specs...  29.8 us
    pallas_call x1, Pallas kernels, fused(): pl.pallas_call(settle, out_shape=out_shape, in_specs=[far, far], out_spec...  1.67 us

profile of v1, /device:TPU:0, one launch (start us, length us, event | category | flops | bytes accessed | tf_op | source)
XLA Modules:
  0.0 32.1 jit_solution(7932107367354752715)
XLA Ops:
  0.6 29.8 %shard_map.86 = (bf16[1,100,8,128]{3,2,1,0:T(8,128)(2,1)}, f32[48,512]{1,0:T(8,128)}) custom-call(s32[1,4,8]{2,1,0:T(4,128)} %lists_hbm.1, s32[1,4]{1,0:T(1,128)} %counts_hbm.1, s32[8,8]{1,0:T(8,128)} %slots_hbm.1, bf16[1,100,32,128]{3,2,1,0:T(8,128)(2,1)} %bitcast.2, bf16[8,8,128,128]{3,2,1,0:T(8,128)(2,1)} %weights_hbm.1, bf16[384,1536]{1,0:T(8,128)(2,1)} %edge_hbm.1, ...), custom_call_target="tpu_custom_call" | custom-call | tf_op jit(solution)/shard_map/pallas_call | solution.py:247
  30.4 1.7 %shard_map.87 = (bf16[1,100,8,128]{3,2,1,0:T(8,128)(2,1)}, f32[48,512]{1,0:T(8,128)}) custom-call(bf16[1,100,8,128]{3,2,1,0:T(8,128)(2,1)} %get-tuple-element.6.hidden, f32[48,512]{1,0:T(8,128)} %get-tuple-element.7.grad), custom_call_target="tpu_custom_call" | custom-call | tf_op jit(solution)/shard_map/pallas_call | solution.py:291

commit v2 on v1

--- a/solution.py
+++ b/solution.py
@@ -36,12 +36,22 @@
     return (hidden, weight_grad)
 
 
+OCTAVES = 40.0
+LOWEST = 26.0
+STEPS = 32767.0 / OCTAVES
+
+
 def encode(value):
-    return value
+    level = (jnp.log2(jnp.maximum(jnp.abs(value), 2.0**-LOWEST)) + LOWEST) * STEPS
+    code = jnp.minimum(level + 0.5, 32767.0).astype(jnp.int32)
+    return jnp.where(value < 0, -code, code).astype(jnp.int16)
 
 
 def decode(code):
-    return code
+    code = code.astype(jnp.int32)
+    level = jnp.abs(code).astype(jnp.float32)
+    size = jnp.exp2(level * (1.0 / STEPS) - LOWEST)
+    return jnp.where(code > 0, size, jnp.where(code < 0, -size, 0.0))
 
 
 def kernel(
@@ -116,18 +126,38 @@
         copy.start()
         return copy
 
-    a2a = []
-    for k, peer in enumerate((outer, near, inner)):
-        for h in range(pieces):
-            for j in range(h * piece, (h + 1) * piece):
-                outgoing[k, j] = block_for(peer, j)
-            if k == 0 and h == 0:
-                pl.semaphore_wait(barrier, 6)
-            a2a.append(send(
-                outgoing.at[k, pl.ds(h * piece, piece)],
-                pool.at[pl.ds(me * slots_each + h * piece, piece)],
-                a2a_send.at[k, h], a2a_recv.at[me, h], (rep, peer),
-            ))
+    end = (low + high) % 2 == 0
+    middle = (low + high) % 2 == 1
+    peers = (outer, near, inner)
+    late = pieces - 1
+    a2a = {}
+
+    def choose(k, h):
+        for j in range(h * piece, (h + 1) * piece):
+            outgoing[k, j] = block_for(peers[k], j)
+        a2a[k, h] = remote(
+            outgoing.at[k, pl.ds(h * piece, piece)],
+            pool.at[pl.ds(me * slots_each + h * piece, piece)],
+            a2a_send.at[k, h], a2a_recv.at[me, h], (rep, peers[k]),
+        )
+
+    def launch(where, keys):
+        @pl.when(where)
+        def _():
+            for key in keys:
+                a2a[key].start()
+
+    for h in range(pieces):
+        choose(0, h)
+        if h == 0:
+            pl.semaphore_wait(barrier, 6)
+        a2a[0, h].start()
+    for h in range(pieces):
+        choose(2, h)
+        if h < late:
+            a2a[2, h].start()
+        else:
+            launch(end, [(2, h)])
 
     def chunk(flip1, flip2):
         return (b1 + flip1 * (1 - 2 * b1)) * w1 + (b2 + flip2 * (1 - 2 * b2)) * w2
@@ -146,6 +176,9 @@
         to_twin.append(send(
             part.at[k, 1 - core], got1.at[k], s1.at[k], r1.at[k], (twin, me)
         ))
+    for h in range(pieces):
+        choose(1, h)
+    launch(middle, [(1, h) for h in range(pieces)])
     for j in range(slots_each):
         pool[me * slots_each + j] = block_for(me, j)
 
@@ -184,9 +217,11 @@
             outz.append(send(linkz.at[i], gotz.at[i], sz.at[i], rz.at[i], (rep, near)))
         else:
             part[kept[0], core, order[i]] = value
+    launch(end, [(1, h) for h in range(pieces)])
     outz[0].wait_recv()
     linkf[...] = encode(part[kept[0], core, far] + decode(gotz[0]))
     last = send(linkf, gotf, sf, rf, (rep, far))
+    launch(middle, [(2, h) for h in range(late, pieces)])
     outz[1].wait_recv()
     grad[...] = part[kept[0], core, me] + decode(gotz[1])
 
@@ -210,7 +245,7 @@
     grad[...] = grad[...] + decode(gotf[...])
     grad_store = pltpu.make_async_copy(grad, grad_out, load_sem.at[1])
     grad_store.start()
-    for copy in a2a + to_twin + out2 + out3 + outz + [last]:
+    for copy in list(a2a.values()) + to_twin + out2 + out3 + outz + [last]:
         copy.wait_send()
     hidden_store.wait()
     grad_store.wait()
@@ -238,7 +273,7 @@
     rows = n_in // (lax.axis_size("rep") * lax.axis_size("sp"))
     bf16, f32 = jnp.bfloat16, jnp.float32
     dma = pltpu.SemaphoreType.DMA
-    i32, link = jnp.int32, jnp.float32
+    i32, link = jnp.int32, jnp.int16
     far = pl.BlockSpec(memory_space=pl.ANY)
     out_shape = (
         jax.ShapeDtypeStruct((1, channels, tiles, nodes), bf16),

time: 32.3 us -> 28.5 us (0.88)
  Pallas kernels: 31.5 us -> 27.7 us
    pallas_call x1, Pallas kernels: 29.8 us -> 26.1 us  [fused(): pl.pallas_call(kernel, out_shape=out_shape, in_specs=[far] * 7, out_specs...]
where the time goes in v2:
time: 28.5 us; the launch traced here: 28.4 us
  Pallas kernels  27.7 us (97%)
  between operations  0.64 us (2%)
    pallas_call x1, Pallas kernels, fused(): pl.pallas_call(kernel, out_shape=out_shape, in_specs=[far] * 7, out_specs...  26.1 us
    pallas_call x1, Pallas kernels, fused(): pl.pallas_call(settle, out_shape=out_shape, in_specs=[far, far], out_spec...  1.67 us

profile of v2, /device:TPU:0, one launch (start us, length us, event | category | flops | bytes accessed | tf_op | source)
XLA Modules:
  0.0 28.4 jit_solution(4711563707824439326)
XLA Ops:
  0.6 26.1 %shard_map.86 = (bf16[1,100,8,128]{3,2,1,0:T(8,128)(2,1)}, f32[48,512]{1,0:T(8,128)}) custom-call(s32[1,4,8]{2,1,0:T(4,128)} %lists_hbm.1, s32[1,4]{1,0:T(1,128)} %counts_hbm.1, s32[8,8]{1,0:T(8,128)} %slots_hbm.1, bf16[1,100,32,128]{3,2,1,0:T(8,128)(2,1)} %bitcast.2, bf16[8,8,128,128]{3,2,1,0:T(8,128)(2,1)} %weights_hbm.1, bf16[384,1536]{1,0:T(8,128)(2,1)} %edge_hbm.1, ...), custom_call_target="tpu_custom_call" | custom-call | tf_op jit(solution)/shard_map/pallas_call | solution.py:282
  26.7 1.7 %shard_map.87 = (bf16[1,100,8,128]{3,2,1,0:T(8,128)(2,1)}, f32[48,512]{1,0:T(8,128)}) custom-call(bf16[1,100,8,128]{3,2,1,0:T(8,128)(2,1)} %get-tuple-element.6.hidden, f32[48,512]{1,0:T(8,128)} %get-tuple-element.7.grad), custom_call_target="tpu_custom_call" | custom-call | tf_op jit(solution)/shard_map/pallas_call | solution.py:326

commit v3 on v2

--- a/solution.py
+++ b/solution.py
@@ -57,7 +57,7 @@
 def kernel(
     lists_hbm, counts_hbm, slots_hbm, field_hbm, weights_hbm, edge_hbm, cot_hbm,
     hidden_out, grad_out,
-    lists, counts, slots, field, wide, weights, edge, cot, outgoing, pool, tall, hidden, grad,
+    lists, counts, slots, field, wide, weights, edge, cot, stage, outgoing, arrived, pool, tall, hidden, grad,
     part, got1, link2, got2, link3, got3, linkz, gotz, linkf, gotf,
     load_sem, a2a_send, a2a_recv, s1, r1, s2, r2, s3, r3, sz, rz, sf, rf,
 ):
@@ -113,7 +113,7 @@
     def block_for(d, j):
         block = rows[pl.ds(lists[0, d, j], channels, stride=pitch), :]
         block = jnp.where(j < counts[0, d], block, jnp.zeros_like(block))
-        return block.astype(jnp.bfloat16)
+        return block
 
     def remote(src, dst, ssem, rsem, device):
         return pltpu.make_async_remote_copy(
@@ -133,11 +133,11 @@
     a2a = {}
 
     def choose(k, h):
-        for j in range(h * piece, (h + 1) * piece):
-            outgoing[k, j] = block_for(peers[k], j)
+        for n in range(piece):
+            stage[pl.ds(n, channels, stride=piece), :] = block_for(peers[k], h * piece + n)
+        outgoing[k, h] = stage[...].astype(outgoing.dtype)
         a2a[k, h] = remote(
-            outgoing.at[k, pl.ds(h * piece, piece)],
-            pool.at[pl.ds(me * slots_each + h * piece, piece)],
+            outgoing.at[k, h], arrived.at[me, h],
             a2a_send.at[k, h], a2a_recv.at[me, h], (rep, peers[k]),
         )
 
@@ -180,7 +180,7 @@
         choose(1, h)
     launch(middle, [(1, h) for h in range(pieces)])
     for j in range(slots_each):
-        pool[me * slots_each + j] = block_for(me, j)
+        pool[me * slots_each + j] = block_for(me, j).astype(pool.dtype)
 
     order = [diag, near, far, me]
     both, crossed, after, kept = (0, 0), (2, 1), (1, 2), (3, 3)
@@ -188,35 +188,47 @@
     def folded(mine, theirs, i):
         return part[mine, core, order[i]] + got1[theirs, order[i]]
 
-    out2 = []
-    for n, k in enumerate((both, crossed)):
-        to_twin[k[1]].wait_recv()
-        for i in range(4):
-            link2[n, i] = encode(folded(*k, i))
-            out2.append(send(
-                link2.at[n, i], got2.at[n, i], s2.at[n, i], r2.at[n, i], (first, me)
-            ))
-    to_twin[after[1]].wait_recv()
-    out3 = []
-    for i in range(4):
+    out2, out3, outz = {}, {}, {}
+
+    def hand_first(n, which, i):
+        link2[n, i] = encode(folded(*which, i))
+        out2[n, i] = send(
+            link2.at[n, i], got2.at[n, i], s2.at[n, i], r2.at[n, i], (first, me)
+        )
+
+    def hand_second(i):
         value = folded(*after, i)
-        out2[i].wait_recv()
+        out2[0, i].wait_recv()
         link3[i] = encode(value + decode(got2[0, i]))
-        out3.append(send(link3.at[i], got3.at[i], s3.at[i], r3.at[i], (second, me)))
-    to_twin[kept[1]].wait_recv()
-    outz = []
-    totals = []
-    for i in range(4):
+        out3[i] = send(link3.at[i], got3.at[i], s3.at[i], r3.at[i], (second, me))
+
+    def gathered(i):
         value = folded(*kept, i)
-        out2[4 + i].wait_recv()
+        out2[1, i].wait_recv()
         value = value + decode(got2[1, i])
         out3[i].wait_recv()
-        value = value + decode(got3[i])
-        if i < 2:
-            linkz[i] = encode(value)
-            outz.append(send(linkz.at[i], gotz.at[i], sz.at[i], rz.at[i], (rep, near)))
-        else:
-            part[kept[0], core, order[i]] = value
+        return value + decode(got3[i])
+
+    to_twin[both[1]].wait_recv()
+    hand_first(0, both, 0)
+    hand_first(0, both, 1)
+    to_twin[crossed[1]].wait_recv()
+    hand_first(1, crossed, 0)
+    hand_first(1, crossed, 1)
+    to_twin[after[1]].wait_recv()
+    hand_second(0)
+    hand_second(1)
+    for i in (2, 3):
+        hand_first(0, both, i)
+        hand_first(1, crossed, i)
+    to_twin[kept[1]].wait_recv()
+    hand_second(2)
+    hand_second(3)
+    for i in (0, 1):
+        linkz[i] = encode(gathered(i))
+        outz[i] = send(linkz.at[i], gotz.at[i], sz.at[i], rz.at[i], (rep, near))
+    for i in (2, 3):
+        part[kept[0], core, order[i]] = gathered(i)
     launch(end, [(1, h) for h in range(pieces)])
     outz[0].wait_recv()
     linkf[...] = encode(part[kept[0], core, far] + decode(gotz[0]))
@@ -227,10 +239,15 @@
 
     slots_load.wait()
     weights_load.wait()
-    for peer in (near, far, diag):
-        for h in range(pieces):
-            ready = pool.at[pl.ds(peer * slots_each + h * piece, piece)]
-            remote(ready, ready, a2a_send.at[0, h], a2a_recv.at[peer, h], (rep, peer)).wait_recv()
+    for k, h in [(k, h) for k in range(3) for h in range(pieces)]:
+        ready = arrived.at[peers[k], h]
+        remote(
+            ready, ready, a2a_send.at[k, h], a2a_recv.at[peers[k], h], (rep, peers[k])
+        ).wait_recv()
+        stage[...] = arrived[peers[k], h].astype(jnp.float32)
+        for n in range(piece):
+            block = stage[pl.ds(n, channels, stride=piece), :]
+            pool[peers[k] * slots_each + h * piece + n] = block.astype(pool.dtype)
     for t in range(tiles):
         left = jnp.concatenate([pool[slots[t, b]] for b in range(reads)], axis=1)
         right = weights[t].reshape(reads * weights.shape[2], weights.shape[3])
@@ -245,7 +262,10 @@
     grad[...] = grad[...] + decode(gotf[...])
     grad_store = pltpu.make_async_copy(grad, grad_out, load_sem.at[1])
     grad_store.start()
-    for copy in list(a2a.values()) + to_twin + out2 + out3 + outz + [last]:
+    for copies in (a2a, out2, out3, outz):
+        for copy in copies.values():
+            copy.wait_send()
+    for copy in to_twin + [last]:
         copy.wait_send()
     hidden_store.wait()
     grad_store.wait()
@@ -293,7 +313,9 @@
             pltpu.VMEM(regrid_weights.shape, bf16),
             pltpu.VMEM(edge_inputs.shape, bf16),
             pltpu.VMEM(cotangent.shape, bf16),
-            pltpu.VMEM((3, slots_each, channels, cells), bf16),
+            pltpu.VMEM((slots_each // 2 * channels, cells), f32),
+            pltpu.VMEM((3, 2, slots_each // 2 * channels, cells), bf16),
+            pltpu.VMEM((4, 2, slots_each // 2 * channels, cells), bf16),
             pltpu.VMEM((4 * slots_each, channels, cells), bf16),
             pltpu.VMEM((channels * tiles, nodes), f32),
             pltpu.VMEM((channels, tiles, nodes), bf16),

time: 28.5 us -> 27.8 us (0.975)
  the two profiles are of different devices: /device:TPU:0 before, /device:TPU:14 now
where the time goes in v3:
time: 27.8 us; the launch traced here: 27.6 us
  Pallas kernels  27 us (97%)
  between operations  0.64 us (2%)
    pallas_call x1, Pallas kernels, fused(): pl.pallas_call(kernel, out_shape=out_shape, in_specs=[far] * 7, out_specs...  25.3 us
    pallas_call x1, Pallas kernels, fused(): pl.pallas_call(settle, out_shape=out_shape, in_specs=[far, far], out_spec...  1.67 us

profile of v3, /device:TPU:14, one launch (start us, length us, event | category | flops | bytes accessed | tf_op | source)
XLA Modules:
  0.0 27.6 jit_solution(8215038749063767220)
XLA Ops:
  0.6 25.3 %shard_map.86 = (bf16[1,100,8,128]{3,2,1,0:T(8,128)(2,1)}, f32[48,512]{1,0:T(8,128)}) custom-call(s32[1,4,8]{2,1,0:T(4,128)} %lists_hbm.1, s32[1,4]{1,0:T(1,128)} %counts_hbm.1, s32[8,8]{1,0:T(8,128)} %slots_hbm.1, bf16[1,100,32,128]{3,2,1,0:T(8,128)(2,1)} %bitcast.2, bf16[8,8,128,128]{3,2,1,0:T(8,128)(2,1)} %weights_hbm.1, bf16[384,1536]{1,0:T(8,128)(2,1)} %edge_hbm.1, ...), custom_call_target="tpu_custom_call" | custom-call | tf_op jit(solution)/shard_map/pallas_call | solution.py:302
  26.0 1.7 %shard_map.87 = (bf16[1,100,8,128]{3,2,1,0:T(8,128)(2,1)}, f32[48,512]{1,0:T(8,128)}) custom-call(bf16[1,100,8,128]{3,2,1,0:T(8,128)(2,1)} %get-tuple-element.6.hidden, f32[48,512]{1,0:T(8,128)} %get-tuple-element.7.grad), custom_call_target="tpu_custom_call" | custom-call | tf_op jit(solution)/shard_map/pallas_call | solution.py:348

commit v4 on v3

--- a/solution.py
+++ b/solution.py
@@ -55,9 +55,9 @@
 
 
 def kernel(
-    lists_hbm, counts_hbm, slots_hbm, field_hbm, weights_hbm, edge_hbm, cot_hbm,
-    hidden_out, grad_out,
-    lists, counts, slots, field, wide, weights, edge, cot, stage, outgoing, arrived, pool, tall, hidden, grad,
+    table_hbm, field_hbm, weights_hbm, edge_hbm, cot_hbm,
+    hidden, grad,
+    table, field, wide, weights, edge, cot, stage, outgoing, arrived, pool, tall,
     part, got1, link2, got2, link3, got3, linkz, gotz, linkf, gotf,
     load_sem, a2a_send, a2a_recv, s1, r1, s2, r2, s3, r3, sz, rz, sf, rf,
 ):
@@ -79,24 +79,21 @@
     outer, inner = 3 * (1 - high), 2 - high
     channels, blocks, cells = field.shape
     pitch = wide.shape[1]
-    slots_each = lists.shape[2]
-    tiles, reads = slots.shape
+    tiles, reads, slots_each = hidden.shape[2], weights.shape[1], table.shape[1]
     width = edge_hbm.shape[1] // 4
     pieces = 2
     piece = slots_each // pieces
 
     loads = [
         pltpu.make_async_copy(field_hbm.at[0], field, load_sem.at[0]),
-        pltpu.make_async_copy(lists_hbm, lists, load_sem.at[4]),
-        pltpu.make_async_copy(counts_hbm, counts, load_sem.at[5]),
+        pltpu.make_async_copy(table_hbm, table, load_sem.at[4]),
         pltpu.make_async_copy(edge_hbm, edge, load_sem.at[1]),
         pltpu.make_async_copy(cot_hbm, cot, load_sem.at[2]),
-        pltpu.make_async_copy(slots_hbm, slots, load_sem.at[6]),
         pltpu.make_async_copy(weights_hbm, weights, load_sem.at[3]),
     ]
     for load in loads:
         load.start()
-    field_load, lists_load, counts_load, edge_load, cot_load, slots_load, weights_load = loads
+    field_load, table_load, edge_load, cot_load, weights_load = loads
 
     barrier = pltpu.get_barrier_semaphore()
     for peer in (far, diag, near):
@@ -107,12 +104,11 @@
     field_load.wait()
     wide[:, :blocks, :] = field[...].astype(jnp.float32)
     rows = wide.reshape(channels * pitch, cells)
-    lists_load.wait()
-    counts_load.wait()
+    table_load.wait()
 
     def block_for(d, j):
-        block = rows[pl.ds(lists[0, d, j], channels, stride=pitch), :]
-        block = jnp.where(j < counts[0, d], block, jnp.zeros_like(block))
+        block = rows[pl.ds(table[d, j], channels, stride=pitch), :]
+        block = jnp.where(j < table[4 + tiles, d], block, jnp.zeros_like(block))
         return block
 
     def remote(src, dst, ssem, rsem, device):
@@ -237,7 +233,6 @@
     outz[1].wait_recv()
     grad[...] = part[kept[0], core, me] + decode(gotz[1])
 
-    slots_load.wait()
     weights_load.wait()
     for k, h in [(k, h) for k in range(3) for h in range(pieces)]:
         ready = arrived.at[peers[k], h]
@@ -249,38 +244,28 @@
             block = stage[pl.ds(n, channels, stride=piece), :]
             pool[peers[k] * slots_each + h * piece + n] = block.astype(pool.dtype)
     for t in range(tiles):
-        left = jnp.concatenate([pool[slots[t, b]] for b in range(reads)], axis=1)
+        left = jnp.concatenate([pool[table[4 + t, b]] for b in range(reads)], axis=1)
         right = weights[t].reshape(reads * weights.shape[2], weights.shape[3])
         tall[pl.ds(t, channels, stride=tiles), :] = jnp.dot(
             left, right, preferred_element_type=jnp.float32
         )
-    hidden[...] = tall[...].reshape(hidden.shape).astype(hidden.dtype)
-    hidden_store = pltpu.make_async_copy(hidden, hidden_out.at[0], load_sem.at[0])
-    hidden_store.start()
+    hidden[0] = tall[...].reshape(hidden.shape[1:]).astype(hidden.dtype)
 
     last.wait_recv()
     grad[...] = grad[...] + decode(gotf[...])
-    grad_store = pltpu.make_async_copy(grad, grad_out, load_sem.at[1])
-    grad_store.start()
     for copies in (a2a, out2, out3, outz):
         for copy in copies.values():
             copy.wait_send()
     for copy in to_twin + [last]:
         copy.wait_send()
-    hidden_store.wait()
-    grad_store.wait()
-
-
-def settle(hidden, grad, hidden_out, grad_out, hidden_held, grad_held, sem):
-    pairs = ((hidden, hidden_held, hidden_out), (grad, grad_held, grad_out))
-    inward = [pltpu.make_async_copy(a, b, sem.at[0, i]) for i, (a, b, _) in enumerate(pairs)]
-    outward = [pltpu.make_async_copy(b, c, sem.at[1, i]) for i, (_, b, c) in enumerate(pairs)]
-    for copy in inward:
+
+
+def settle(hidden, grad, hidden_out, grad_out, sem):
+    pairs = ((hidden, hidden_out), (grad, grad_out))
+    copies = [pltpu.make_async_copy(a, b, sem.at[i]) for i, (a, b) in enumerate(pairs)]
+    for copy in copies:
         copy.start()
-    for i in range(2):
-        inward[i].wait()
-        outward[i].start()
-    for copy in outward:
+    for copy in copies:
         copy.wait()
 
 
@@ -295,19 +280,23 @@
     dma = pltpu.SemaphoreType.DMA
     i32, link = jnp.int32, jnp.int16
     far = pl.BlockSpec(memory_space=pl.ANY)
+    near = pl.BlockSpec(memory_space=pltpu.VMEM)
     out_shape = (
         jax.ShapeDtypeStruct((1, channels, tiles, nodes), bf16),
         jax.ShapeDtypeStruct((rows, hid), f32),
     )
+    shards = send_blocks.shape[1]
+    width = max(slots_each, tile_slot.shape[1], shards)
+    table = jnp.pad(send_blocks[0], ((0, tiles + 1), (0, width - slots_each)))
+    table += jnp.pad(tile_slot, ((shards, 1), (0, width - tile_slot.shape[1])))
+    table += jnp.pad(send_count, ((shards + tiles, 0), (0, width - shards)))
     hidden, grad = pl.pallas_call(
         kernel,
         out_shape=out_shape,
-        in_specs=[far] * 7,
-        out_specs=(far, far),
+        in_specs=[far] * 5,
+        out_specs=(near, near),
         scratch_shapes=[
-            pltpu.SMEM(send_blocks.shape, i32),
-            pltpu.SMEM(send_count.shape, i32),
-            pltpu.SMEM(tile_slot.shape, i32),
+            pltpu.SMEM(table.shape, i32),
             pltpu.VMEM((channels, blocks, cells), bf16),
             pltpu.VMEM((channels, blocks + 8, cells), f32),
             pltpu.VMEM(regrid_weights.shape, bf16),
@@ -318,8 +307,6 @@
             pltpu.VMEM((4, 2, slots_each // 2 * channels, cells), bf16),
             pltpu.VMEM((4 * slots_each, channels, cells), bf16),
             pltpu.VMEM((channels * tiles, nodes), f32),
-            pltpu.VMEM((channels, tiles, nodes), bf16),
-            pltpu.VMEM((rows, hid), f32),
             pltpu.VMEM((4, 2, 4, rows, hid), f32),
             pltpu.VMEM((4, 4, rows, hid), f32),
             pltpu.VMEM((2, 4, rows, hid), link),
@@ -339,18 +326,16 @@
             dma, dma,
         ],
         compiler_params=pltpu.CompilerParams(
-            collective_id=0, has_side_effects=True, vmem_limit_bytes=56 * 1024 * 1024
+            collective_id=0, has_side_effects=True, vmem_limit_bytes=56000000
         ),
     )(
-        send_blocks, send_count, tile_slot, jnp.transpose(field, (0, 2, 1, 3)),
+        table, jnp.transpose(field, (0, 2, 1, 3)),
         regrid_weights, edge_inputs, cotangent,
     )
     hidden, grad = pl.pallas_call(
-        settle, out_shape=out_shape, in_specs=[far, far], out_specs=(far, far),
-        scratch_shapes=[
-            pltpu.VMEM(out_shape[0].shape, bf16), pltpu.VMEM(out_shape[1].shape, f32), dma((2, 2)),
-        ],
-        compiler_params=pltpu.CompilerParams(vmem_limit_bytes=57000 * 1024),
+        settle, out_shape=out_shape, in_specs=[near, near], out_specs=(far, far),
+        scratch_shapes=[dma((2,))],
+        compiler_params=pltpu.CompilerParams(vmem_limit_bytes=2 * 1024 * 1024),
     )(hidden, grad)
     return jnp.transpose(hidden, (0, 2, 1, 3)), grad
 

time: 27.8 us -> 27.1 us (0.975)
  the two profiles are of different devices: /device:TPU:14 before, /device:TPU:0 now
where the time goes in v4:
time: 27.1 us; the launch traced here: 26.9 us
  Pallas kernels  25.5 us (94%)
  other arithmetic  0.72 us (3%)
  between operations  0.64 us (2%)
    pallas_call x1, Pallas kernels, fused(): pl.pallas_call(kernel, out_shape=out_shape, in_specs=[far] * 5, out_specs...  24.8 us
    pallas_call x1, Pallas kernels, fused(): pl.pallas_call(settle, out_shape=out_shape, in_specs=[near, near], out_sp...  0.73 us
    add x1, other arithmetic, fused(): table += jnp.pad(send_count, ((shards + tiles, 0), (0, width - shards)))  0.72 us

profile of v4, /device:TPU:0, one launch (start us, length us, event | category | flops | bytes accessed | tf_op | source)
XLA Modules:
  0.0 26.9 jit_solution(13878490890654575953)
XLA Ops:
  0.6 0.7 %pad_add_fusion.table_hbm = s32[13,8]{1,0:T(8,128)S(1)} fusion(s32[1,4]{1,0:T(1,128)} %param.9, s32[8,8]{1,0:T(8,128)} %param.11, s32[4,8]{1,0:T(4,128)} %bitcast.4), kind=kLoop, calls=%fused_computation | loop fusion | flops 208 | bytes 816 | tf_op jit(solution)/shard_map/add | solution.py:292
  1.4 24.8 %shard_map.86 = (bf16[1,100,8,128]{3,2,1,0:T(8,128)(2,1)S(1)}, f32[48,512]{1,0:T(8,128)S(1)}) custom-call(s32[13,8]{1,0:T(8,128)S(1)} %pad_add_fusion.table_hbm, bf16[1,100,32,128]{3,2,1,0:T(8,128)(2,1)} %bitcast.3, bf16[8,8,128,128]{3,2,1,0:T(8,128)(2,1)} %weights_hbm.1, bf16[384,1536]{1,0:T(8,128)(2,1)} %edge_hbm.1, bf16[384,512]{1,0:T(8,128)(2,1)} %cot_hbm.1), custom_call_target="tpu_custom_call" | custom-call | tf_op jit(solution)/shard_map/pallas_call | solution.py:293
  26.1 0.7 %shard_map.87 = (bf16[1,100,8,128]{3,2,1,0:T(8,128)(2,1)}, f32[48,512]{1,0:T(8,128)}) custom-call(bf16[1,100,8,128]{3,2,1,0:T(8,128)(2,1)S(1)} %get-tuple-element.6.hidden, f32[48,512]{1,0:T(8,128)S(1)} %get-tuple-element.7.grad), custom_call_target="tpu_custom_call" | custom-call | tf_op jit(solution)/shard_map/pallas_call | solution.py:335

commit v5 on v4

--- a/solution.py
+++ b/solution.py
@@ -42,8 +42,8 @@
 
 
 def encode(value):
-    level = (jnp.log2(jnp.maximum(jnp.abs(value), 2.0**-LOWEST)) + LOWEST) * STEPS
-    code = jnp.minimum(level + 0.5, 32767.0).astype(jnp.int32)
+    level = jnp.log2(jnp.abs(value)) * STEPS + (LOWEST * STEPS + 0.5)
+    code = jnp.clip(level, 0.0, 32767.0).astype(jnp.int32)
     return jnp.where(value < 0, -code, code).astype(jnp.int16)
 
 
@@ -79,10 +79,11 @@
     outer, inner = 3 * (1 - high), 2 - high
     channels, blocks, cells = field.shape
     pitch = wide.shape[1]
-    tiles, reads, slots_each = hidden.shape[2], weights.shape[1], table.shape[1]
+    tiles, reads = hidden.shape[2], weights.shape[1]
     width = edge_hbm.shape[1] // 4
     pieces = 2
-    piece = slots_each // pieces
+    piece = stage.shape[0] // channels
+    slots_each = piece * pieces
 
     loads = [
         pltpu.make_async_copy(field_hbm.at[0], field, load_sem.at[0]),
@@ -211,12 +212,12 @@
     to_twin[crossed[1]].wait_recv()
     hand_first(1, crossed, 0)
     hand_first(1, crossed, 1)
+    for i in (2, 3):
+        hand_first(0, both, i)
+        hand_first(1, crossed, i)
     to_twin[after[1]].wait_recv()
     hand_second(0)
     hand_second(1)
-    for i in (2, 3):
-        hand_first(0, both, i)
-        hand_first(1, crossed, i)
     to_twin[kept[1]].wait_recv()
     hand_second(2)
     hand_second(3)

time: 27.1 us -> 27 us (level)
  no operation moved by 1% of the time
where the time goes in v5:
time: 27 us; the launch traced here: 26.7 us
  Pallas kernels  25.3 us (94%)
  other arithmetic  0.72 us (3%)
  between operations  0.64 us (2%)
    pallas_call x1, Pallas kernels, fused(): pl.pallas_call(kernel, out_shape=out_shape, in_specs=[far] * 5, out_specs...  24.6 us
    pallas_call x1, Pallas kernels, fused(): pl.pallas_call(settle, out_shape=out_shape, in_specs=[near, near], out_sp...  0.73 us
    add x1, other arithmetic, fused(): table += jnp.pad(send_count, ((shards + tiles, 0), (0, width - shards)))  0.72 us

profile of v5, /device:TPU:0, one launch (start us, length us, event | category | flops | bytes accessed | tf_op | source)
XLA Modules:
  0.0 26.7 jit_solution(5328198161846550891)
XLA Ops:
  0.6 0.7 %pad_add_fusion.table_hbm = s32[13,8]{1,0:T(8,128)S(1)} fusion(s32[1,4]{1,0:T(1,128)} %param.9, s32[8,8]{1,0:T(8,128)} %param.11, s32[4,8]{1,0:T(4,128)} %bitcast.4), kind=kLoop, calls=%fused_computation | loop fusion | flops 208 | bytes 816 | tf_op jit(solution)/shard_map/add | solution.py:293
  1.4 24.6 %shard_map.86 = (bf16[1,100,8,128]{3,2,1,0:T(8,128)(2,1)S(1)}, f32[48,512]{1,0:T(8,128)S(1)}) custom-call(s32[13,8]{1,0:T(8,128)S(1)} %pad_add_fusion.table_hbm, bf16[1,100,32,128]{3,2,1,0:T(8,128)(2,1)} %bitcast.3, bf16[8,8,128,128]{3,2,1,0:T(8,128)(2,1)} %weights_hbm.1, bf16[384,1536]{1,0:T(8,128)(2,1)} %edge_hbm.1, bf16[384,512]{1,0:T(8,128)(2,1)} %cot_hbm.1), custom_call_target="tpu_custom_call" | custom-call | tf_op jit(solution)/shard_map/pallas_call | solution.py:294
  26.0 0.7 %shard_map.87 = (bf16[1,100,8,128]{3,2,1,0:T(8,128)(2,1)}, f32[48,512]{1,0:T(8,128)}) custom-call(bf16[1,100,8,128]{3,2,1,0:T(8,128)(2,1)S(1)} %get-tuple-element.6.hidden, f32[48,512]{1,0:T(8,128)S(1)} %get-tuple-element.7.grad), custom_call_target="tpu_custom_call" | custom-call | tf_op jit(solution)/shard_map/pallas_call | solution.py:336

commit v6 on v5

--- a/solution.py
+++ b/solution.py
@@ -59,7 +59,7 @@
     hidden, grad,
     table, field, wide, weights, edge, cot, stage, outgoing, arrived, pool, tall,
     part, got1, link2, got2, link3, got3, linkz, gotz, linkf, gotf,
-    load_sem, a2a_send, a2a_recv, s1, r1, s2, r2, s3, r3, sz, rz, sf, rf,
+    load_sem, a2a_send, a2a_recv, s1, r1, s2, r2, s3, r3, sz, rz, sf, rf, ready,
 ):
     rep = lax.axis_index("rep")
     me = lax.axis_index("sp")
@@ -76,7 +76,8 @@
     near = 2 * high + 1 - low
     far = 2 * (1 - high) + low
     diag = 2 * (1 - high) + 1 - low
-    outer, inner = 3 * (1 - high), 2 - high
+    ahead, behind = 2 * (1 - high), 3 - 2 * high
+    last_shard = me == 3
     channels, blocks, cells = field.shape
     pitch = wide.shape[1]
     tiles, reads = hidden.shape[2], weights.shape[1]
@@ -97,8 +98,11 @@
     field_load, table_load, edge_load, cot_load, weights_load = loads
 
     barrier = pltpu.get_barrier_semaphore()
-    for peer in (far, diag, near):
-        pl.semaphore_signal(barrier, inc=1, device_id=(rep, peer), device_id_type=MESH)
+    @pl.when(jnp.logical_not(last_shard))
+    def _():
+        for peer in (far, diag, near):
+            pl.semaphore_signal(barrier, inc=1, device_id=(rep, peer), device_id_type=MESH)
+
     for peer in (twin, first, second):
         pl.semaphore_signal(barrier, inc=1, device_id=(peer, me), device_id_type=MESH)
 
@@ -125,8 +129,8 @@
 
     end = (low + high) % 2 == 0
     middle = (low + high) % 2 == 1
-    peers = (outer, near, inner)
-    late = pieces - 1
+    upper, lower = high == 1, high == 0
+    peers = (ahead, near, behind)
     a2a = {}
 
     def choose(k, h):
@@ -144,17 +148,21 @@
             for key in keys:
                 a2a[key].start()
 
-    for h in range(pieces):
-        choose(0, h)
-        if h == 0:
-            pl.semaphore_wait(barrier, 6)
-        a2a[0, h].start()
-    for h in range(pieces):
-        choose(2, h)
-        if h < late:
-            a2a[2, h].start()
-        else:
-            launch(end, [(2, h)])
+    choose(0, 0)
+    pl.semaphore_wait(barrier, 5 + me // 3)
+
+    @pl.when(last_shard)
+    def _():
+        for peer in (far, diag, near):
+            pl.semaphore_signal(ready, inc=1, device_id=(rep, peer), device_id_type=MESH)
+
+    a2a[0, 0].start()
+    choose(0, 1)
+    a2a[0, 1].start()
+    choose(2, 0)
+    launch(upper, [(2, 0)])
+    choose(2, 1)
+    launch(last_shard & (core == 0), [(2, 1)])
 
     def chunk(flip1, flip2):
         return (b1 + flip1 * (1 - 2 * b1)) * w1 + (b2 + flip2 * (1 - 2 * b2)) * w2
@@ -175,7 +183,7 @@
         ))
     for h in range(pieces):
         choose(1, h)
-    launch(middle, [(1, h) for h in range(pieces)])
+    launch(middle & lower, [(1, h) for h in range(pieces)])
     for j in range(slots_each):
         pool[me * slots_each + j] = block_for(me, j).astype(pool.dtype)
 
@@ -206,6 +214,13 @@
         out3[i].wait_recv()
         return value + decode(got3[i])
 
+    @pl.when(jnp.logical_not(last_shard))
+    def _():
+        pl.semaphore_wait(ready, 1)
+
+    launch(lower, [(2, 0)])
+    launch(end & lower, [(2, 1)])
+    launch(middle & upper, [(1, h) for h in range(pieces)])
     to_twin[both[1]].wait_recv()
     hand_first(0, both, 0)
     hand_first(0, both, 1)
@@ -226,11 +241,13 @@
         outz[i] = send(linkz.at[i], gotz.at[i], sz.at[i], rz.at[i], (rep, near))
     for i in (2, 3):
         part[kept[0], core, order[i]] = gathered(i)
+    launch(last_shard & (core == 1), [(2, 1)])
     launch(end, [(1, h) for h in range(pieces)])
     outz[0].wait_recv()
     linkf[...] = encode(part[kept[0], core, far] + decode(gotz[0]))
     last = send(linkf, gotf, sf, rf, (rep, far))
-    launch(middle, [(2, h) for h in range(late, pieces)])
+    launch(middle & upper, [(2, 1)])
+    launch(middle & lower, [(2, 1)])
     outz[1].wait_recv()
     grad[...] = part[kept[0], core, me] + decode(gotz[1])
 
@@ -325,6 +342,7 @@
             dma((4,)), dma((4,)),
             dma((2,)), dma((2,)),
             dma, dma,
+            pltpu.SemaphoreType.REGULAR,
         ],
         compiler_params=pltpu.CompilerParams(
             collective_id=0, has_side_effects=True, vmem_limit_bytes=56000000

time: 27 us -> 27.1 us (level)
  the two profiles are of different devices: /device:TPU:0 before, /device:TPU:14 now
where the time goes in v6:
time: 27.1 us; the launch traced here: 26.9 us
  Pallas kernels  25.6 us (94%)
  other arithmetic  0.72 us (3%)
  between operations  0.64 us (2%)
    pallas_call x1, Pallas kernels, fused(): pl.pallas_call(kernel, out_shape=out_shape, in_specs=[far] * 5, out_specs...  24.8 us
    pallas_call x1, Pallas kernels, fused(): pl.pallas_call(settle, out_shape=out_shape, in_specs=[near, near], out_sp...  0.73 us
    add x1, other arithmetic, fused(): table += jnp.pad(send_count, ((shards + tiles, 0), (0, width - shards)))  0.72 us

profile of v6, /device:TPU:14, one launch (start us, length us, event | category | flops | bytes accessed | tf_op | source)
XLA Modules:
  0.0 26.9 jit_solution(5833509014567473842)
XLA Ops:
  0.6 0.7 %pad_add_fusion.table_hbm = s32[13,8]{1,0:T(8,128)S(1)} fusion(s32[1,4]{1,0:T(1,128)} %param.9, s32[8,8]{1,0:T(8,128)} %param.11, s32[4,8]{1,0:T(4,128)} %bitcast.4), kind=kLoop, calls=%fused_computation | loop fusion | flops 208 | bytes 816 | tf_op jit(solution)/shard_map/add | solution.py:310
  1.4 24.8 %shard_map.86 = (bf16[1,100,8,128]{3,2,1,0:T(8,128)(2,1)S(1)}, f32[48,512]{1,0:T(8,128)S(1)}) custom-call(s32[13,8]{1,0:T(8,128)S(1)} %pad_add_fusion.table_hbm, bf16[1,100,32,128]{3,2,1,0:T(8,128)(2,1)} %bitcast.3, bf16[8,8,128,128]{3,2,1,0:T(8,128)(2,1)} %weights_hbm.1, bf16[384,1536]{1,0:T(8,128)(2,1)} %edge_hbm.1, bf16[384,512]{1,0:T(8,128)(2,1)} %cot_hbm.1), custom_call_target="tpu_custom_call" | custom-call | tf_op jit(solution)/shard_map/pallas_call | solution.py:311
  26.2 0.7 %shard_map.87 = (bf16[1,100,8,128]{3,2,1,0:T(8,128)(2,1)}, f32[48,512]{1,0:T(8,128)}) custom-call(bf16[1,100,8,128]{3,2,1,0:T(8,128)(2,1)S(1)} %get-tuple-element.6.hidden, f32[48,512]{1,0:T(8,128)S(1)} %get-tuple-element.7.grad), custom_call_target="tpu_custom_call" | custom-call | tf_op jit(solution)/shard_map/pallas_call | solution.py:354
